TPU v7x, 32 devices: a whole 2x2x4 slice. The times are simulated.
32 devices in a mesh: fsdp: 4 (over y, x), tp: 8 (over z, core).
Axes of the slice: x: 2, y: 2, z: 4, core: 2. Of those that a mesh axis runs over, the one named last changes fastest.
Arguments:
- tokens: bfloat16 [1024, 8192], P('fsdp', 'tp'), may hold values from -6 to 6
- out_grad: bfloat16 [1024, 8192], P('fsdp', 'tp'), may hold values from -6 to 6
- gate_weight: bfloat16 [8192, 1024], P('fsdp', 'tp'), may hold values from -0.0625 to 0.0625
- up_weight: bfloat16 [8192, 1024], P('fsdp', 'tp'), may hold values from -0.0625 to 0.0625
- down_weight: bfloat16 [1024, 8192], P('tp', 'fsdp'), may hold values from -0.1875 to 0.1875
Outputs:
- input_grad: bfloat16 [1024, 8192], P('fsdp', 'tp')
- gate_grad: float32 [8192, 1024], P('fsdp', 'tp')
- up_grad: float32 [8192, 1024], P('fsdp', 'tp')
- down_grad: float32 [1024, 8192], P('tp', 'fsdp')
All inputs are finite; a program needn't handle non-finite values.
Results may differ from a plain program's by a relative error of at most 0.0023.
Values may be sent and summed in bfloat16 or wider, within the bound.
A program may use at most 128 MiB of HBM per device.

v0:
```python
import math
import jax
import jax.numpy as jnp
from jax import lax
from jax.sharding import PartitionSpec as P


def over_all(shard, axis, dim, absorb, state):
    everything = jax.tree.map(lambda a: lax.all_gather(a, axis, axis=dim, tiled=True), shard)
    return absorb(state, everything, jnp.int32(0))


def own_rows(portion, rows, axis):
    count = rows * lax.axis_size(axis)
    return lax.psum_scatter(portion(jnp.int32(0), count), axis, scatter_dimension=0, tiled=True)


def column_term(left, right, start, count, factor):
    block = lax.dynamic_slice_in_dim(left, start, count, 1)
    product = lax.dot_general(
        block, right, (((0,), (0,)), ((), ())), preferred_element_type=jnp.float32
    )
    return product * factor


def body(tokens, out_grad, gate_weight, up_weight, down_weight):
    factor = 1.0 / math.sqrt(tokens.shape[0] * lax.axis_size("fsdp"))
    whole = lax.all_gather(tokens, "tp", axis=1, tiled=True)
    grads = lax.all_gather(out_grad, "tp", axis=1, tiled=True)
    gate_full, up_full = (
        lax.all_gather(gate_weight, "fsdp", axis=0, tiled=True),
        lax.all_gather(up_weight, "fsdp", axis=0, tiled=True),
    )
    gate = jnp.dot(whole, gate_full, preferred_element_type=jnp.float32)
    up = jnp.dot(whole, up_full, preferred_element_type=jnp.float32)

    def add_down(total, piece, start):
        columns = lax.dynamic_slice_in_dim(grads, start, piece.shape[1], 1)
        return total + lax.dot_general(
            columns, piece, (((1,), (1,)), ((), ())), preferred_element_type=jnp.float32
        )

    initial = jnp.zeros((whole.shape[0], down_weight.shape[0]), jnp.float32)
    hidden_grad = over_all(down_weight, "fsdp", 1, add_down, initial)
    squashed = jax.nn.sigmoid(gate)
    activated = gate * squashed
    slope = squashed * (1.0 + gate * (1.0 - squashed))
    hidden = (activated * up).astype(jnp.bfloat16)
    gate_delta = (hidden_grad * up * slope).astype(jnp.bfloat16)
    up_delta = (hidden_grad * activated).astype(jnp.bfloat16)
    partial_term = jnp.dot(gate_delta, gate_full.T, preferred_element_type=jnp.float32)
    partial_term = partial_term + jnp.dot(up_delta, up_full.T, preferred_element_type=jnp.float32)
    input_grad = lax.psum_scatter(partial_term, "tp", scatter_dimension=1, tiled=True).astype(
        jnp.bfloat16
    )
    rows_here = gate_weight.shape[0]

    def joint_term(start, count):
        return jnp.concatenate(
            [
                column_term(whole, gate_delta, start, count, factor),
                column_term(whole, up_delta, start, count, factor),
                column_term(grads, hidden, start, count, factor),
            ],
            axis=1,
        )

    summed = own_rows(joint_term, rows_here, "fsdp")
    width = gate_delta.shape[1]
    gate_grad = summed[:, :width]
    up_grad = summed[:, width : 2 * width]
    down_grad = summed[:, 2 * width :].T
    return (input_grad, gate_grad, up_grad, down_grad)


def solution(mesh):
    return jax.shard_map(
        body,
        mesh=mesh,
        in_specs=(
            P("fsdp", "tp"),
            P("fsdp", "tp"),
            P("fsdp", "tp"),
            P("fsdp", "tp"),
            P("tp", "fsdp"),
        ),
        out_specs=(P("fsdp", "tp"), P("fsdp", "tp"), P("fsdp", "tp"), P("tp", "fsdp")),
        check_vma=False,
    )
```

profile of v0, /device:TPU:0, one launch (start us, length us, event | category | flops | bytes accessed | tf_op | source)
XLA Modules:
  0.0 450.8 jit_solution(9459281939705098741)
XLA Ops:
  7.2 0.0 all-gather.14.cloned.1.call-start
  7.2 0.7 all-gather.14.cloned.1.call-update
  7.9 0.0 all-gather.10.cloned.1.call-start
  7.9 0.7 all-gather.10.cloned.1.call-update
  8.6 0.0 all-gather.12.cloned.1.call-start
  8.7 0.7 all-gather.12.cloned.1.call-update
  9.4 0.0 all-gather.8.cloned.1.call-start
  9.4 0.5 all-gather.8.cloned.1.call-update
  10.0 0.0 all-gather.6.cloned.1.call-start
  10.0 0.5 all-gather.6.cloned.1.call-update
  10.5 0.0 reduce-scatter.3.cloned.1.call-start
  10.6 37.2 %all-gather.14.cloned.1.call-done = bf16[8192,128]{1,0:T(8,128)(2,1)} async-done(((bf16[2048,128]{1,0:T(8,128)(2,1)}), bf16[8192,128]{1,0:T(8,128)(2,1)}) %all-gather.14.cloned.1.call-update) | async-done | bytes 2097168 | tf_op jit(solution)/shard_map/all_gather | solution.py:31
  47.8 48.5 %all-gather.10.cloned.1.call-done = bf16[256,8192]{1,0:T(8,128)(2,1)} async-done(((bf16[256,1024]{1,0:T(8,128)(2,1)}), bf16[256,8192]{1,0:T(8,128)(2,1)}) %all-gather.10.cloned.1.call-update) | async-done | bytes 4194320 | tf_op jit(solution)/shard_map/all_gather | solution.py:28
  96.3 4.1 fusion.7
  100.4 31.8 %all-gather.12.cloned.1.call-done = bf16[8192,128]{1,0:T(8,128)(2,1)} async-done(((bf16[2048,128]{1,0:T(8,128)(2,1)}), bf16[8192,128]{1,0:T(8,128)(2,1)}) %all-gather.12.cloned.1.call-update) | async-done | bytes 2097168 | tf_op jit(solution)/shard_map/all_gather | solution.py:32
  132.1 4.1 fusion.6
  136.2 0.0 copy-start.1
  136.2 32.8 %all-gather.8.cloned.1.call-done = bf16[128,8192]{1,0:T(8,128)(2,1)} async-done(((bf16[128,2048]{1,0:T(8,128)(2,1)}), bf16[128,8192]{1,0:T(8,128)(2,1)}) %all-gather.8.cloned.1.call-update) | async-done | bytes 2097168 | tf_op jit(solution)/shard_map/all_gather | solution.py:9
  169.0 48.4 %all-gather.6.cloned.1.call-done = bf16[256,8192]{1,0:T(8,128)(2,1)} async-done(((bf16[256,1024]{1,0:T(8,128)(2,1)}), bf16[256,8192]{1,0:T(8,128)(2,1)}) %all-gather.6.cloned.1.call-update) | async-done | bytes 4194320 | tf_op jit(solution)/shard_map/all_gather | solution.py:29
  217.4 4.1 multiply_convert_fusion.1
  221.5 0.0 copy-done.1
  221.5 0.0 copy-start.2
  221.5 1.3 fusion.8
  222.8 0.3 copy-done.2
  223.1 4.5 convolution_add_fusion
  227.6 0.0 reduce-scatter.3.cloned.1.call-update
  227.6 0.0 reduce-scatter.5.cloned.1.call-start
  227.6 0.0 copy-start
  227.6 3.1 fusion.1
  230.8 0.3 copy-done
  231.1 0.0 copy-start.3
  231.1 0.8 fusion.2
  231.9 2.1 copy-done.3
  234.0 0.8 fusion
  234.8 5.0 %pad_maximum_fusion = f32[8192,384]{0,1:T(8,128)} fusion(f32[8192,128]{0,1:T(8,128)S(1)} %fusion, f32[8192,128]{0,1:T(8,128)S(1)} %fusion.1, f32[8192,128]{0,1:T(8,128)S(1)} %fusion.2), kind=kLoop, calls=%fused_computation | loop fusion | flops 6291456 | bytes 25165824 | tf_op jit(solution)/shard_map/concatenate | solution.py:59
  239.8 0.0 reduce-scatter.5.cloned.1.call-update
  239.9 76.2 %reduce-scatter.3.cloned.1.call-done = f32[256,1024]{1,0:T(8,128)} async-done(((f32[256,8192]{1,0:T(8,128)}), f32[256,1024]{1,0:T(8,128)}) %reduce-scatter.3.cloned.1.call-update) | async-done | bytes 1048592 | tf_op jit(solution)/shard_map/reduce_scatter | solution.py:53
  316.1 2.1 convert_element_type.14
  318.2 120.1 %reduce-scatter.5.cloned.1.call-done = f32[2048,384]{0,1:T(8,128)} async-done(((f32[8192,384]{0,1:T(8,128)}), f32[2048,384]{0,1:T(8,128)}) %reduce-scatter.5.cloned.1.call-update) | async-done | bytes 3145744 | tf_op jit(solution)/shard_map/reduce_scatter | solution.py:15
  438.3 3.1 slice_bitcast_fusion
  441.4 1.3 copy.9
  442.7 1.3 copy.10
Async XLA Ops:
  7.2 40.6 %all-gather.14.cloned.1.call-start = ((), (), s32[]{:S(2)}) async-start(), calls=%async_computation.6 | async-start | bytes 2621440 | tf_op jit(solution)/shard_map/all_gather | solution.py:31
  7.9 88.4 %all-gather.10.cloned.1.call-start = ((), (), s32[]{:S(2)}) async-start(), calls=%async_computation.4 | async-start | bytes 4718592 | tf_op jit(solution)/shard_map/all_gather | solution.py:28
  8.6 123.5 %all-gather.12.cloned.1.call-start = ((), (), s32[]{:S(2)}) async-start(), calls=%async_computation.5 | async-start | bytes 2621440 | tf_op jit(solution)/shard_map/all_gather | solution.py:32
  9.4 159.6 %all-gather.8.cloned.1.call-start = ((), (), s32[]{:S(2)}) async-start(), calls=%async_computation.3 | async-start | bytes 2621440 | tf_op jit(solution)/shard_map/all_gather | solution.py:9
  10.0 207.4 %all-gather.6.cloned.1.call-start = ((), (), s32[]{:S(2)}) async-start(), calls=%async_computation.2 | async-start | bytes 4718592 | tf_op jit(solution)/shard_map/all_gather | solution.py:29
  10.5 305.5 %reduce-scatter.3.cloned.1.call-start = ((), (), s32[]{:S(2)}) async-start(), calls=%async_computation.7 | async-start | bytes 9437184 | tf_op jit(solution)/shard_map/reduce_scatter | solution.py:53
  136.2 85.3 %copy-start.1 = (bf16[8192,128]{1,0:T(8,128)(2,1)S(1)}, bf16[8192,128]{1,0:T(8,128)(2,1)}, u32[]{:S(2)}) copy-start(bf16[8192,128]{1,0:T(8,128)(2,1)} %all-gather.14.cloned.1.call-done) | copy-start | bytes 6291460
  221.5 1.6 copy-start.2
  227.6 210.7 %reduce-scatter.5.cloned.1.call-start = ((), (), s32[]{:S(2)}) async-start(), calls=%async_computation.8 | async-start | bytes 15728640 | tf_op jit(solution)/shard_map/reduce_scatter | solution.py:15
  227.6 3.5 copy-start
  231.1 2.9 copy-start.3
Sparse Core Ops, SparseCore 0:
  9.8 37.8 all-gather.13
  49.4 46.8 all-gather.9
  98.1 33.9 all-gather.11
  133.8 35.1 all-gather.7
  170.5 46.8 all-gather.5
  227.7 88.3 reduce-scatter.2
  319.2 119.0 reduce-scatter.4
where the time goes:
time: 451 us
  waiting for transfers between devices  398 us (88%)
  matrix products  22.8 us (5%)
  between operations  14.2 us (3%)
  local copies, waits for them, and re-layouts  8.46 us (2%)
  other arithmetic  7.1 us (2%)
    reduce_scatter x1, waiting for transfers between devices, own_rows(): lax.psum_scatter(portion(jnp.int32(0), count), axis, scatter_dimension=0,...  120 us
    reduce_scatter x1, waiting for transfers between devices, body(): lax.psum_scatter(partial_term, 'tp', scatter_dimension=1, tiled=True)  76.2 us
    all_gather x1, waiting for transfers between devices, body(): whole = lax.all_gather(tokens, 'tp', axis=1, tiled=True)  48.5 us
    all_gather x1, waiting for transfers between devices, body(): grads = lax.all_gather(out_grad, 'tp', axis=1, tiled=True)  48.4 us
    all_gather x1, waiting for transfers between devices, body(): lax.all_gather(gate_weight, 'fsdp', axis=0, tiled=True)  37.2 us
    all_gather x1, waiting for transfers between devices, over_all(): lax.all_gather(a, axis, axis=dim, tiled=True)  32.8 us
    all_gather x1, waiting for transfers between devices, body(): lax.all_gather(up_weight, 'fsdp', axis=0, tiled=True)  31.8 us
  transfers between devices with their start and end apart: 7, of which 7 were waited for; matrix products, arithmetic and copies ran while one was open for 4% of the time, Pallas kernels for 0%

commit v1 on v0

--- a/solution.py
+++ b/solution.py
@@ -25,7 +25,12 @@
 
 def body(tokens, out_grad, gate_weight, up_weight, down_weight):
     factor = 1.0 / math.sqrt(tokens.shape[0] * lax.axis_size("fsdp"))
-    whole = lax.all_gather(tokens, "tp", axis=1, tiled=True)
+    ring = [tokens]
+    for hop in range(7):
+        ring.append(lax.ppermute(ring[-1], "tp", [(dev, (dev + 1) % 8) for dev in range(8)]))
+    whole = jnp.roll(
+        jnp.concatenate(ring[::-1], axis=1), (lax.axis_index("tp") + 1) * ring[0].shape[1], axis=1
+    )
     grads = lax.all_gather(out_grad, "tp", axis=1, tiled=True)
     gate_full, up_full = (
         lax.all_gather(gate_weight, "fsdp", axis=0, tiled=True),

time: 451 us -> 404 us (0.90)
  waiting for transfers between devices: 398 us -> 331 us
  local copies, waits for them, and re-layouts: 8.46 us -> 23.6 us
    ppermute x0 -> x7, waiting for transfers between devices: none -> 73.9 us  [body(): lax.ppermute(ring[-1], 'tp', [(dev, (dev + 1) % 8) for dev in range(8)])]
    all_gather x1 -> x0, waiting for transfers between devices: 48.5 us -> none  [body(): whole = lax.all_gather(tokens, 'tp', axis=1, tiled=True)]
    all_gather x1, waiting for transfers between devices: 37.2 us -> 0.01 us  [body(): lax.all_gather(gate_weight, 'fsdp', axis=0, tiled=True)]
    all_gather x1, waiting for transfers between devices: 31.8 us -> 0.02 us  [body(): lax.all_gather(up_weight, 'fsdp', axis=0, tiled=True)]
    all_gather x1, waiting for transfers between devices: 32.8 us -> 10.8 us  [over_all(): lax.all_gather(a, axis, axis=dim, tiled=True)]
    unnamed x10 -> x25, local copies, waits for them, and re-layouts: 5.38 us -> 19.6 us
  transfers between devices with their start and end apart: 7 -> 13, of which waited for: 7 -> 11; matrix products, arithmetic and copies ran while one was open for 4% -> 10% of each run, Pallas kernels for 0% -> 0%
where the time goes in v1:
time: 404 us; the launch traced here: 403 us
  waiting for transfers between devices  331 us (82%)
  matrix products  26.3 us (7%)
  local copies, waits for them, and re-layouts  23.6 us (6%)
  between operations  14.2 us (4%)
  other arithmetic  7.03 us (2%)
    reduce_scatter x1, waiting for transfers between devices, own_rows(): lax.psum_scatter(portion(jnp.int32(0), count), axis, scatter_dimension=0,...  120 us
    reduce_scatter x1, waiting for transfers between devices, body(): lax.psum_scatter(partial_term, 'tp', scatter_dimension=1, tiled=True)  75.8 us
    ppermute x7, waiting for transfers between devices, body(): lax.ppermute(ring[-1], 'tp', [(dev, (dev + 1) % 8) for dev in range(8)])  73.9 us
    all_gather x1, waiting for transfers between devices, body(): grads = lax.all_gather(out_grad, 'tp', axis=1, tiled=True)  48.4 us
    unnamed x25, local copies, waits for them, and re-layouts  19.6 us
    all_gather x1, waiting for transfers between devices, over_all(): lax.all_gather(a, axis, axis=dim, tiled=True)  10.8 us
  transfers between devices with their start and end apart: 13, of which 11 were waited for; matrix products, arithmetic and copies ran while one was open for 10% of the time, Pallas kernels for 0%

profile of v1, /device:TPU:0, one launch (start us, length us, event | category | flops | bytes accessed | tf_op | source)
XLA Modules:
  0.0 403.3 jit_solution(2693401050739954374)
XLA Ops:
  7.2 0.0 copy-start.3
  7.2 0.0 all-gather.11.cloned.1.call-start
  7.2 0.7 all-gather.11.cloned.1.call-update
  7.9 0.0 all-gather.9.cloned.1.call-start
  8.0 0.7 all-gather.9.cloned.1.call-update
  8.7 0.0 all-gather.7.cloned.1.call-start
  8.7 0.7 all-gather.7.cloned.1.call-update
  9.4 0.0 all-gather.5.cloned.1.call-start
  9.4 0.5 all-gather.5.cloned.1.call-update
  10.0 0.0 reduce-scatter.3.cloned.1.call-start
  10.0 0.5 collective-permute-start
  10.6 11.1 %collective-permute-done = bf16[256,1024]{1,0:T(8,128)(2,1)S(1)} collective-permute-done((bf16[256,1024]{1,0:T(8,128)(2,1)}, bf16[256,1024]{1,0:T(8,128)(2,1)S(1)}, u32[]{:S(2)}, u32[]{:S(2)}) %collective-permute-start) | collective-permute-done | bytes 524320 | tf_op jit(solution)/shard_map/ppermute | solution.py:30
  21.7 0.0 collective-permute-start.1
  21.7 10.4 %collective-permute-done.1 = bf16[256,1024]{1,0:T(8,128)(2,1)S(1)} collective-permute-done((bf16[256,1024]{1,0:T(8,128)(2,1)S(1)}, bf16[256,1024]{1,0:T(8,128)(2,1)S(1)}, u32[]{:S(2)}, u32[]{:S(2)}) %collective-permute-start.1) | collective-permute-done | bytes 524320 | tf_op jit(solution)/shard_map/ppermute | solution.py:30
  32.1 0.0 collective-permute-start.2
  32.1 10.4 %collective-permute-done.2 = bf16[256,1024]{1,0:T(8,128)(2,1)S(1)} collective-permute-done((bf16[256,1024]{1,0:T(8,128)(2,1)S(1)}, bf16[256,1024]{1,0:T(8,128)(2,1)S(1)}, u32[]{:S(2)}, u32[]{:S(2)}) %collective-permute-start.2) | collective-permute-done | bytes 524320 | tf_op jit(solution)/shard_map/ppermute | solution.py:30
  42.5 0.0 collective-permute-start.3
  42.5 10.4 %collective-permute-done.3 = bf16[256,1024]{1,0:T(8,128)(2,1)S(1)} collective-permute-done((bf16[256,1024]{1,0:T(8,128)(2,1)S(1)}, bf16[256,1024]{1,0:T(8,128)(2,1)S(1)}, u32[]{:S(2)}, u32[]{:S(2)}) %collective-permute-start.3) | collective-permute-done | bytes 524320 | tf_op jit(solution)/shard_map/ppermute | solution.py:30
  52.9 0.0 collective-permute-start.4
  52.9 10.4 %collective-permute-done.4 = bf16[256,1024]{1,0:T(8,128)(2,1)S(1)} collective-permute-done((bf16[256,1024]{1,0:T(8,128)(2,1)S(1)}, bf16[256,1024]{1,0:T(8,128)(2,1)S(1)}, u32[]{:S(2)}, u32[]{:S(2)}) %collective-permute-start.4) | collective-permute-done | bytes 524320 | tf_op jit(solution)/shard_map/ppermute | solution.py:30
  63.3 0.0 collective-permute-start.5
  63.3 10.5 %collective-permute-done.5 = bf16[256,1024]{1,0:T(8,128)(2,1)} collective-permute-done((bf16[256,1024]{1,0:T(8,128)(2,1)S(1)}, bf16[256,1024]{1,0:T(8,128)(2,1)}, u32[]{:S(2)}, u32[]{:S(2)}) %collective-permute-start.5) | collective-permute-done | bytes 524320 | tf_op jit(solution)/shard_map/ppermute | solution.py:30
  73.8 0.0 collective-permute-start.6
  73.8 10.7 %collective-permute-done.6 = bf16[256,1024]{1,0:T(8,128)(2,1)} collective-permute-done((bf16[256,1024]{1,0:T(8,128)(2,1)}, bf16[256,1024]{1,0:T(8,128)(2,1)}, u32[]{:S(2)}, u32[]{:S(2)}) %collective-permute-start.6) | collective-permute-done | bytes 524320 | tf_op jit(solution)/shard_map/ppermute | solution.py:30
  84.5 1.9 constant_dynamic-update-slice_fusion.15
  86.4 1.9 constant_dynamic-update-slice_fusion.14
  88.3 0.8 constant_dynamic-update-slice_fusion.13
  89.1 0.8 constant_dynamic-update-slice_fusion.12
  90.0 0.9 constant_dynamic-update-slice_fusion.11
  90.8 0.8 constant_dynamic-update-slice_fusion.10
  91.7 0.9 constant_dynamic-update-slice_fusion.9
  92.5 0.0 copy-done.3
  92.5 0.9 constant_dynamic-update-slice_fusion.8
  93.4 2.0 constant_dynamic-update-slice_fusion.7
  95.4 1.9 constant_dynamic-update-slice_fusion.6
  97.3 0.8 constant_dynamic-update-slice_fusion.5
  98.1 0.8 constant_dynamic-update-slice_fusion.4
  99.0 0.8 constant_dynamic-update-slice_fusion.3
  99.8 0.9 constant_dynamic-update-slice_fusion.2
  100.7 0.9 constant_dynamic-update-slice_fusion.1
  101.5 0.8 constant_dynamic-update-slice_fusion
  102.4 4.2 %fusion.3 = f32[256,128]{1,0:T(8,128)S(1)} fusion(bf16[8192,128]{1,0:T(8,128)(2,1)} %all-gather.11.cloned.1.call-done, bf16[256,16384]{1,0:T(8,128)(2,1)} %constant_dynamic-update-slice_fusion, s32[]{:T(128)S(6)} %select_n.14), kind=kOutput, calls=%fused_computation.8 | convolution fusion | flops 536870912 | bytes 6422532 | tf_op jit(solution)/shard_map/dot_general | solution.py:39
  106.6 0.0 all-gather.9.cloned.1.call-done
  106.6 4.5 %fusion.5 = f32[256,128]{1,0:T(8,128)S(1)} fusion(bf16[8192,128]{1,0:T(8,128)(2,1)} %all-gather.9.cloned.1.call-done, bf16[256,16384]{1,0:T(8,128)(2,1)} %constant_dynamic-update-slice_fusion, s32[]{:T(128)S(6)} %select_n.14), kind=kOutput, calls=%fused_computation.10 | convolution fusion | flops 536870912 | bytes 6422532 | tf_op jit(solution)/shard_map/dot_general | solution.py:40
  111.1 10.8 %all-gather.7.cloned.1.call-done = bf16[128,8192]{1,0:T(8,128)(2,1)} async-done(((bf16[128,2048]{1,0:T(8,128)(2,1)}), bf16[128,8192]{1,0:T(8,128)(2,1)}) %all-gather.7.cloned.1.call-update) | async-done | bytes 2097168 | tf_op jit(solution)/shard_map/all_gather | solution.py:9
  121.9 48.4 %all-gather.5.cloned.1.call-done = bf16[256,8192]{1,0:T(8,128)(2,1)} async-done(((bf16[256,1024]{1,0:T(8,128)(2,1)}), bf16[256,8192]{1,0:T(8,128)(2,1)}) %all-gather.5.cloned.1.call-update) | async-done | bytes 4194320 | tf_op jit(solution)/shard_map/all_gather | solution.py:34
  170.2 4.2 %multiply_convert_fusion.1 = (bf16[256,128]{1,0:T(8,128)(2,1)S(1)}, bf16[256,128]{1,0:T(8,128)(2,1)S(1)}) fusion(f32[256,128]{1,0:T(8,128)S(1)} %fusion.3, f32[256,128]{1,0:T(8,128)S(1)} %fusion.5, bf16[256,8192]{1,0:T(8,128)(2,1)} %all-gather.5.cloned.1.call-done, bf16[128,8192]{1,0:T(8,128)(2,1)} %all-gather.7.cloned.1.call-done), kind=kOutput, calls=%fused_computation.14 | convolution fusion | flops 537296896 | bytes 6684672 | tf_op jit(solution)/shard_map/dot_general | solution.py:44
  174.5 0.0 copy-done
  174.5 1.3 fusion.14
  175.8 0.0 copy-done.1
  175.8 4.5 %convolution_add_fusion = f32[256,8192]{1,0:T(8,128)} fusion(f32[256,8192]{1,0:T(8,128)S(1)} %fusion.14, bf16[256,128]{1,0:T(8,128)(2,1)S(1)} %get-tuple-element.11, bf16[8192,128]{1,0:T(8,128)(2,1)S(1)} %copy-done.1), kind=kOutput, calls=%fused_computation.1 | convolution fusion | flops 538968064 | bytes 18939904 | tf_op jit(solution)/shard_map/dot_general | solution.py:57
  180.2 0.0 reduce-scatter.3.cloned.1.call-update
  180.2 0.0 reduce-scatter.5.cloned.1.call-start
  180.3 3.2 convolution_multiply_fusion.1
  183.5 3.6 convolution_multiply_fusion.2
  187.1 0.8 fusion
  187.9 4.9 %pad_maximum_fusion = f32[8192,384]{0,1:T(8,128)} fusion(f32[8192,128]{0,1:T(8,128)S(1)} %fusion, f32[8192,128]{0,1:T(8,128)S(1)} %convolution_multiply_fusion.1, f32[8192,128]{0,1:T(8,128)S(1)} %convolution_multiply_fusion.2), kind=kLoop, calls=%fused_computation | loop fusion | flops 6291456 | bytes 25165824 | tf_op jit(solution)/shard_map/concatenate | solution.py:64
  192.9 0.0 reduce-scatter.5.cloned.1.call-update
  192.9 75.8 %reduce-scatter.3.cloned.1.call-done = f32[256,1024]{1,0:T(8,128)} async-done(((f32[256,8192]{1,0:T(8,128)}), f32[256,1024]{1,0:T(8,128)}) %reduce-scatter.3.cloned.1.call-update) | async-done | bytes 1048592 | tf_op jit(solution)/shard_map/reduce_scatter | solution.py:58
  268.7 2.1 convert_element_type.14
  270.8 120.0 %reduce-scatter.5.cloned.1.call-done = f32[2048,384]{0,1:T(8,128)} async-done(((f32[8192,384]{0,1:T(8,128)}), f32[2048,384]{0,1:T(8,128)}) %reduce-scatter.5.cloned.1.call-update) | async-done | bytes 3145744 | tf_op jit(solution)/shard_map/reduce_scatter | solution.py:15
  390.8 3.1 slice_bitcast_fusion
  393.9 1.3 copy.9
  395.2 1.3 copy.10
  (5 shorter events, 0.0 us)
Async XLA Ops:
  7.2 85.4 %copy-start.3 = (bf16[256,1024]{1,0:T(8,128)(2,1)S(1)}, bf16[256,1024]{1,0:T(8,128)(2,1)}, u32[]{:S(2)}) copy-start(bf16[256,1024]{1,0:T(8,128)(2,1)} %param.5) | copy-start | bytes 1572868
  7.2 95.2 %all-gather.11.cloned.1.call-start = ((), (), s32[]{:S(2)}) async-start(), calls=%async_computation.5 | async-start | bytes 2621440 | tf_op jit(solution)/shard_map/all_gather | solution.py:36
  7.9 98.7 %all-gather.9.cloned.1.call-start = ((), (), s32[]{:S(2)}) async-start(), calls=%async_computation.4 | async-start | bytes 2621440 | tf_op jit(solution)/shard_map/all_gather | solution.py:37
  8.7 113.2 %all-gather.7.cloned.1.call-start = ((), (), s32[]{:S(2)}) async-start(), calls=%async_computation.3 | async-start | bytes 2621440 | tf_op jit(solution)/shard_map/all_gather | solution.py:9
  9.4 160.8 %all-gather.5.cloned.1.call-start = ((), (), s32[]{:S(2)}) async-start(), calls=%async_computation.2 | async-start | bytes 4718592 | tf_op jit(solution)/shard_map/all_gather | solution.py:34
  10.0 258.8 %reduce-scatter.3.cloned.1.call-start = ((), (), s32[]{:S(2)}) async-start(), calls=%async_computation.6 | async-start | bytes 9437184 | tf_op jit(solution)/shard_map/reduce_scatter | solution.py:58
  10.0 11.6 %collective-permute-start = (bf16[256,1024]{1,0:T(8,128)(2,1)}, bf16[256,1024]{1,0:T(8,128)(2,1)S(1)}, u32[]{:S(2)}, u32[]{:S(2)}) collective-permute-start(bf16[256,1024]{1,0:T(8,128)(2,1)} %param.5), channel_id=1, source_target_pairs={{0,1},{1,2},{2,3},{3,4},{4,5},{5,6},{6,7},{7,0},{8,9},{9,10},{10,1... | collective-permute-start | bytes 1572872 | tf_op jit(solution)/shard_map/ppermute | solution.py:30
  21.7 10.4 %collective-permute-start.1 = (bf16[256,1024]{1,0:T(8,128)(2,1)S(1)}, bf16[256,1024]{1,0:T(8,128)(2,1)S(1)}, u32[]{:S(2)}, u32[]{:S(2)}) collective-permute-start(bf16[256,1024]{1,0:T(8,128)(2,1)S(1)} %collective-permute-done), channel_id=1, source_target_pairs={{0,1},{1,2},{2,3},{3,4},{4,5},{5,6},{6,7},{7,0},{8,9},{9,10},{10,1... | collective-permute-start | bytes 1572872 | tf_op jit(solution)/shard_map/ppermute | solution.py:30
  32.1 10.4 %collective-permute-start.2 = (bf16[256,1024]{1,0:T(8,128)(2,1)S(1)}, bf16[256,1024]{1,0:T(8,128)(2,1)S(1)}, u32[]{:S(2)}, u32[]{:S(2)}) collective-permute-start(bf16[256,1024]{1,0:T(8,128)(2,1)S(1)} %collective-permute-done.1), channel_id=1, source_target_pairs={{0,1},{1,2},{2,3},{3,4},{4,5},{5,6},{6,7},{7,0},{8,9},{9,10},{10,1... | collective-permute-start | bytes 1572872 | tf_op jit(solution)/shard_map/ppermute | solution.py:30
  42.5 10.4 %collective-permute-start.3 = (bf16[256,1024]{1,0:T(8,128)(2,1)S(1)}, bf16[256,1024]{1,0:T(8,128)(2,1)S(1)}, u32[]{:S(2)}, u32[]{:S(2)}) collective-permute-start(bf16[256,1024]{1,0:T(8,128)(2,1)S(1)} %collective-permute-done.2), channel_id=1, source_target_pairs={{0,1},{1,2},{2,3},{3,4},{4,5},{5,6},{6,7},{7,0},{8,9},{9,10},{10,1... | collective-permute-start | bytes 1572872 | tf_op jit(solution)/shard_map/ppermute | solution.py:30
  52.9 10.4 %collective-permute-start.4 = (bf16[256,1024]{1,0:T(8,128)(2,1)S(1)}, bf16[256,1024]{1,0:T(8,128)(2,1)S(1)}, u32[]{:S(2)}, u32[]{:S(2)}) collective-permute-start(bf16[256,1024]{1,0:T(8,128)(2,1)S(1)} %collective-permute-done.3), channel_id=1, source_target_pairs={{0,1},{1,2},{2,3},{3,4},{4,5},{5,6},{6,7},{7,0},{8,9},{9,10},{10,1... | collective-permute-start | bytes 1572872 | tf_op jit(solution)/shard_map/ppermute | solution.py:30
  63.3 10.5 %collective-permute-start.5 = (bf16[256,1024]{1,0:T(8,128)(2,1)S(1)}, bf16[256,1024]{1,0:T(8,128)(2,1)}, u32[]{:S(2)}, u32[]{:S(2)}) collective-permute-start(bf16[256,1024]{1,0:T(8,128)(2,1)S(1)} %collective-permute-done.4), channel_id=1, source_target_pairs={{0,1},{1,2},{2,3},{3,4},{4,5},{5,6},{6,7},{7,0},{8,9},{9,10},{10,1... | collective-permute-start | bytes 1572872 | tf_op jit(solution)/shard_map/ppermute | solution.py:30
  73.8 10.7 %collective-permute-start.6 = (bf16[256,1024]{1,0:T(8,128)(2,1)}, bf16[256,1024]{1,0:T(8,128)(2,1)}, u32[]{:S(2)}, u32[]{:S(2)}) collective-permute-start(bf16[256,1024]{1,0:T(8,128)(2,1)} %collective-permute-done.5), channel_id=1, source_target_pairs={{0,1},{1,2},{2,3},{3,4},{4,5},{5,6},{6,7},{7,0},{8,9},{9,10},{10,1... | collective-permute-start | bytes 1572872 | tf_op jit(solution)/shard_map/ppermute | solution.py:30
  102.4 72.1 %copy-start = (bf16[8192,128]{1,0:T(8,128)(2,1)S(1)}, bf16[8192,128]{1,0:T(8,128)(2,1)}, u32[]{:S(2)}) copy-start(bf16[8192,128]{1,0:T(8,128)(2,1)} %all-gather.11.cloned.1.call-done) | copy-start | bytes 6291460
  170.2 5.5 %copy-start.1 = (bf16[8192,128]{1,0:T(8,128)(2,1)S(1)}, bf16[8192,128]{1,0:T(8,128)(2,1)}, u32[]{:S(2)}) copy-start(bf16[8192,128]{1,0:T(8,128)(2,1)} %all-gather.9.cloned.1.call-done) | copy-start | bytes 6291460
  180.2 210.5 %reduce-scatter.5.cloned.1.call-start = ((), (), s32[]{:S(2)}) async-start(), calls=%async_computation.7 | async-start | bytes 15728640 | tf_op jit(solution)/shard_map/reduce_scatter | solution.py:15
  180.3 6.8 %copy-start.2 = (bf16[256,8192]{1,0:T(8,128)(2,1)S(1)}, bf16[256,8192]{1,0:T(8,128)(2,1)}, u32[]{:S(2)}) copy-start(bf16[256,8192]{1,0:T(8,128)(2,1)} %all-gather.5.cloned.1.call-done) | copy-start | bytes 12582916
Sparse Core Ops, SparseCore 0:
  9.8 37.8 all-gather.10
  49.6 35.1 all-gather.8
  86.7 35.1 all-gather.6
  123.3 46.8 all-gather.4
  180.4 88.3 reduce-scatter.2
  271.7 119.0 reduce-scatter.4
